TPU v7x, 32 devices: a whole 2x2x4 slice. The times are simulated.
32 devices in a mesh: groups: 1, ctx: 32 (over z, y, x, core).
Axes of the slice: x: 2, y: 2, z: 4, core: 2. Of those that a mesh axis runs over, the one named last changes fastest.
Arguments:
- prefill_query: bfloat16 [1024, 32, 576], P('groups', 'ctx'), may hold values from -1000 to 1000
- prefill_latent: bfloat16 [1024, 576], P(('groups', 'ctx')), may hold values from -6 to 6
- decode_query: bfloat16 [2, 32, 576], P('groups'), may hold values from -1000 to 1000
- cache: bfloat16 [2, 16384, 576], P('groups', 'ctx'), may hold values from -6 to 6
- lengths: int32 [2], P('groups'), may hold values from 2049 to 16384
- page_table: int32 [64, 2], P('groups'), may hold values from 0 to 31, as said below
Outputs:
- prefill_out: bfloat16 [1024, 32, 512], P('groups', 'ctx')
- decode_out: bfloat16 [2, 32, 512], P('groups', 'ctx')
Inputs may be any that keep to these rules, and one draw needn't show every extreme that they name: `page_table`: row p names the device (column 0, below 32) and the pool slot (column 1, below 16) that take latent page p; no two rows name the same pair.
All inputs are finite; a program needn't handle non-finite values.
Results may differ from a plain program's by a relative error of at most 0.0049.
Values may be sent and summed in bfloat16 or wider, within the bound.
A program may use at most 64 MiB of HBM per device.

v0:
```python
import jax
import jax.numpy as jnp
from jax import lax
from jax.sharding import PartitionSpec as P

D_LAT = 512
PAGE = 16
POOL = 16
REQ = 2


SCALE = 192.0 ** (-0.5)
NEG = -1e30


def attend_block(state_now, queries, shard_rows, first_row):
    run_max, run_sum, weighted = state_now
    length = shard_rows.shape[0]
    scores = (
        jnp.einsum("ihc,jc->ihj", queries, shard_rows, preferred_element_type=jnp.float32) * SCALE
    )
    row_index = jnp.arange(queries.shape[0], dtype=jnp.int32)
    key_index = first_row + jnp.arange(length, dtype=jnp.int32)
    allowed = (key_index[None, :] <= row_index[:, None])[:, None, :]
    masked = jnp.where(allowed, scores, NEG)
    new_max = jnp.maximum(run_max, jnp.max(masked, axis=2))
    weights = jnp.where(allowed, jnp.exp(scores - new_max[:, :, None]), 0.0)
    factor = jnp.exp(run_max - new_max)
    new_sum = run_sum * factor + jnp.sum(weights, axis=2)
    product = jnp.einsum(
        "ihj,jv->ihv",
        weights.astype(jnp.bfloat16),
        shard_rows[:, :D_LAT],
        preferred_element_type=jnp.float32,
    )
    return (new_max, new_sum, weighted * factor[:, :, None] + product)


def attend_blocks(state_now, queries, shard_rows, first_row):
    length = shard_rows.shape[0]
    block_rows = min(length, 512)
    starts = list(range(0, length, block_rows))
    for start in starts:
        stop = min(start + block_rows, length)
        state_now = attend_block(state_now, queries, shard_rows[start:stop], first_row + start)
    return state_now


def pick_rows(shard_rows, first_row, source_rows, pool_live):
    length = shard_rows.shape[0]
    local_rows = source_rows - first_row
    inside = (local_rows >= 0) & (local_rows < length) & pool_live
    taken = jnp.take(shard_rows, jnp.clip(local_rows, 0, length - 1), axis=0)
    return jnp.where(inside[:, None], taken, jnp.zeros_like(taken))


def shards(prefill_query, prefill_latent, decode_query, cache, lengths, page_table):
    device = lax.axis_index("ctx")
    span = prefill_query.shape[0]
    head_here = prefill_query.shape[1]
    width = prefill_latent.shape[1]
    page_count = page_table.shape[0]
    slot_index = jnp.arange(POOL, dtype=jnp.int32)
    chosen = (page_table[None, :, 0] == device) & (page_table[None, :, 1] == slot_index[:, None])
    slot_live = jnp.any(chosen, axis=1)
    slot_page = jnp.sum(
        jnp.where(chosen, jnp.arange(page_count, dtype=jnp.int32)[None, :], 0), axis=1
    )
    offsets = jnp.arange(PAGE, dtype=jnp.int32)
    source_rows = (slot_page[:, None] * PAGE + offsets[None, :]).reshape(-1)
    pool_live = jnp.repeat(slot_live, PAGE)
    pool_request = jnp.repeat((device * POOL + slot_index) % REQ, PAGE)
    initial = (
        jnp.full((span, head_here), NEG, jnp.float32),
        jnp.zeros((span, head_here), jnp.float32),
        jnp.zeros((span, head_here, D_LAT), jnp.float32),
        jnp.zeros((POOL * PAGE, width), jnp.bfloat16),
    )
    gathered = lax.all_gather(prefill_latent, "ctx", axis=0, tiled=True)
    attended = attend_blocks(initial[:3], prefill_query, gathered, 0)
    final = attended + (pick_rows(gathered, 0, source_rows, pool_live),)
    run_max, run_sum, weighted, pool_rows = final
    prefill_out = (weighted / run_sum[:, :, None]).astype(jnp.bfloat16)
    cache_dev = cache.shape[1]
    positions = device * cache_dev + jnp.arange(cache_dev, dtype=jnp.int32)
    resident_ok = (positions[None, :] < lengths[:, None])[:, None, :]
    resident_scores = (
        jnp.einsum("rhc,rtc->rht", decode_query, cache, preferred_element_type=jnp.float32) * SCALE
    )
    request_index = jnp.arange(REQ, dtype=jnp.int32)
    pool_ok = ((pool_request[None, :] == request_index[:, None]) & pool_live[None, :])[:, None, :]
    pool_scores = (
        jnp.einsum("rhc,kc->rhk", decode_query, pool_rows, preferred_element_type=jnp.float32)
        * SCALE
    )
    part_max = jnp.maximum(
        jnp.max(jnp.where(resident_ok, resident_scores, NEG), axis=2),
        jnp.max(jnp.where(pool_ok, pool_scores, NEG), axis=2),
    )
    resident_weights = jnp.where(resident_ok, jnp.exp(resident_scores - part_max[:, :, None]), 0.0)
    pool_weights = jnp.where(pool_ok, jnp.exp(pool_scores - part_max[:, :, None]), 0.0)
    part_sum = jnp.sum(resident_weights, axis=2) + jnp.sum(pool_weights, axis=2)
    part_out = jnp.einsum(
        "rht,rtv->rhv",
        resident_weights.astype(jnp.bfloat16),
        cache[:, :, :D_LAT],
        preferred_element_type=jnp.float32,
    )
    part_out = part_out + jnp.einsum(
        "rhk,kv->rhv",
        pool_weights.astype(jnp.bfloat16),
        pool_rows[:, :D_LAT],
        preferred_element_type=jnp.float32,
    )
    moved_max, moved_sum, moved_out = (
        lax.all_to_all(part_max[None], "ctx", split_axis=2, concat_axis=0, tiled=True),
        lax.all_to_all(part_sum[None], "ctx", split_axis=2, concat_axis=0, tiled=True),
        lax.all_to_all(part_out[None], "ctx", split_axis=2, concat_axis=0, tiled=True),
    )
    top_all = jnp.max(moved_max, axis=0)
    scales = jnp.exp(moved_max - top_all[None])
    own_sum = jnp.sum(moved_sum * scales, axis=0)
    own_out = jnp.sum(moved_out * scales[..., None], axis=0)
    decode_out = (own_out / own_sum[:, :, None]).astype(jnp.bfloat16)
    return (prefill_out, decode_out)


def solution(mesh):
    in_specs = (
        P("groups", "ctx", None),
        P(("groups", "ctx"), None),
        P("groups", None, None),
        P("groups", "ctx", None),
        P("groups"),
        P("groups", None),
    )
    out_specs = (P("groups", "ctx", None), P("groups", "ctx", None))
    return jax.shard_map(shards, mesh=mesh, in_specs=in_specs, out_specs=out_specs, check_vma=False)
```

profile of v0, /device:TPU:1, one launch (start us, length us, event | category | flops | bytes accessed | tf_op | source)
XLA Modules:
  0.0 113.7 jit_solution(10159602554596118152)
XLA Ops:
  7.2 0.0 copy-start
  7.2 0.0 all-gather.2.cloned.1.call-start
  7.2 0.7 all-gather.2.cloned.1.call-update
  7.9 0.7 slice_bitcast_fusion.2
  8.6 0.7 compare_bitcast_fusion
  9.3 0.1 select_reduce_fusion.4
  9.4 0.1 fusion.41
  9.5 0.1 min.18
  9.6 0.1 min.16
  9.6 0.1 fusion.46
  9.7 0.1 and.59
  9.8 0.1 fusion.45
  9.9 0.1 broadcast_in_dim.129
  10.0 0.1 and.55
  10.1 0.1 broadcast_in_dim.128
  10.2 0.1 eq.50
  10.4 0.7 broadcast_compare_fusion
  11.1 1.7 %select_reduce_fusion.2 = (f32[2,32]{1,0:T(2,128)S(1)}, f32[2,32,512]{2,1,0:T(8,128)S(1)}) fusion(pred[2,512]{1,0:T(4,128)(4,1)S(1)} %broadcast_compare_fusion, bf16[2,32,576]{2,1,0:T(8,128)(2,1)} %param.8, bf16[2,512,576]{1,2,0:T(8,128)(2,1)} %param.9), kind=kOutput, calls=%fused_computation.42 | convolution fusion | flops 37846976 | bytes 1385728 | tf_op jit(solution)/shard_map/rhc,rtc->rht/dot_general | solution.py:88
  12.8 54.8 %all-gather.2.cloned.1.call-done = bf16[1024,576]{1,0:T(8,128)(2,1)} async-done(((bf16[32,576]{1,0:T(8,128)(2,1)}), bf16[1024,576]{1,0:T(8,128)(2,1)}) %all-gather.2.cloned.1.call-update) | async-done | bytes 1179664 | tf_op jit(solution)/shard_map/all_gather | solution.py:79
  67.6 2.9 %gather_fusion = bf16[256,576]{1,0:T(8,128)(2,1)S(1)} fusion(bf16[1024,576]{1,0:T(8,128)(2,1)} %all-gather.2.cloned.1.call-done, s32[1024]{0:T(1024)S(1)} %pad_clamp_fusion), kind=kCustom, calls=%fused_computation | custom fusion | bytes 590848 | tf_op jit(solution)/shard_map/jit(_take)/gather | solution.py:53
  70.5 0.2 select_select_fusion
  70.7 0.3 select_reduce_fusion.3
  71.0 0.2 fusion.27
  71.2 0.2 fusion.35
  71.4 0.7 copy.21
  72.1 3.5 %all-to-all-start.1 = ((f32[1,2,32]{1,0,2:T(1,128)}), f32[1,2,32]{1,0,2:T(1,128)S(1)}, u32[]{:S(2)}, u32[]{:S(2)}) async-start(f32[1,2,32]{1,0,2:T(1,128)} %copy.21), calls=%async_computation.1 | async-start | bytes 32768 | tf_op jit(solution)/shard_map/all_to_all | solution.py:116
  75.6 0.2 fusion.29
  75.8 1.0 select_reduce_fusion.1
  76.8 1.0 select_reduce_fusion
  77.8 0.9 fusion
  78.7 0.8 fusion.12
  79.5 2.1 %fusion.4 = bf16[1024,1,512]{2,0,1:T(8,128)(2,1)} fusion(f32[1024,512]{1,0:T(8,128)S(1)} %fusion.12, f32[1024,512]{0,1:T(8,128)S(1)} %get-tuple-element.10, f32[1024]{0:T(1024)S(1)} %get-tuple-element.2, f32[1024]{0:T(1024)S(1)} %get-tuple-element.5, f32[1024]{0:T(1024)S(1)} %get-tuple-element.3, s32[512]{0:T(512)S(1)} %iota_add_fusion.2, ...), kind=kOutput, calls=%fused_computation.12 | convolution fusion | flops 542113792 | bytes 5785600 | tf_op jit(solution)/shard_map/ihj,jv->ihv/dot_general | solution.py:30
  81.6 0.7 copy.24
  82.3 0.1 all-to-all-done.1
  82.4 5.8 %all-to-all-start.2 = ((f32[1,2,32]{1,0,2:T(1,128)}), f32[1,2,32]{1,0,2:T(1,128)S(1)}, u32[]{:S(2)}, u32[]{:S(2)}) async-start(f32[1,2,32]{1,0,2:T(1,128)} %copy.24), calls=%async_computation.2 | async-start | bytes 32768 | tf_op jit(solution)/shard_map/all_to_all | solution.py:117
  88.1 1.6 %fusion.9 = f32[1,2,32,512]{3,2,1,0:T(8,128)S(1)} fusion(f32[2,32,512]{2,1,0:T(8,128)S(1)} %fusion.27, bf16[2,512,576]{1,2,0:T(8,128)(2,1)} %param.9, f32[2,32,512]{2,1,0:T(8,128)S(1)} %get-tuple-element.12, f32[2,32]{1,0:T(2,128)S(1)} %max.39, pred[2,512]{1,0:T(4,128)(4,1)S(1)} %broadcast_compare_fusion), kind=kOutput, calls=%fused_computation.18 | convolution fusion | flops 33685504 | bytes 1443072 | tf_op jit(solution)/shard_map/rht,rtv->rhv/dot_general | solution.py:103
  89.8 0.8 copy.20
  90.5 0.1 copy.22
  90.6 0.1 reduce_max.49
  90.7 4.3 %all-to-all-done.2 = f32[1,2,32]{1,0,2:T(1,128)S(1)} async-done(((f32[1,2,32]{1,0,2:T(1,128)}), f32[1,2,32]{1,0,2:T(1,128)S(1)}, u32[]{:S(2)}, u32[]{:S(2)}) %all-to-all-start.2) | async-done | bytes 288 | tf_op jit(solution)/shard_map/all_to_all | solution.py:117
  94.9 2.8 %all-to-all-start = ((f32[1,2,32,512]{3,1,0,2:T(2,128)}), f32[1,2,32,512]{3,1,0,2:T(2,128)S(1)}, u32[]{:S(2)}, u32[]{:S(2)}) async-start(f32[1,2,32,512]{3,1,0,2:T(2,128)} %copy.20), calls=%async_computation | async-start | bytes 262144 | tf_op jit(solution)/shard_map/all_to_all | solution.py:118
  97.8 0.1 fusion.51
  97.8 0.1 copy.23
  97.9 0.1 copy.25
  98.0 0.2 fusion.50
  98.2 7.9 %all-to-all-done = f32[1,2,32,512]{3,1,0,2:T(2,128)S(1)} async-done(((f32[1,2,32,512]{3,1,0,2:T(2,128)}), f32[1,2,32,512]{3,1,0,2:T(2,128)S(1)}, u32[]{:S(2)}, u32[]{:S(2)}) %all-to-all-start) | async-done | bytes 131104 | tf_op jit(solution)/shard_map/all_to_all | solution.py:118
  106.1 0.1 fusion.28
  106.2 0.7 fusion.47
  (18 shorter events, 0.1 us)
Async XLA Ops:
  7.2 68.6 %copy-start = (bf16[1024,1,576]{0,2,1:T(8,128)(2,1)S(1)}, bf16[1024,1,576]{0,2,1:T(8,128)(2,1)}, u32[]{:S(2)}) copy-start(bf16[1024,1,576]{0,2,1:T(8,128)(2,1)} %param.6) | copy-start | bytes 3538948
  7.2 60.4 %all-gather.2.cloned.1.call-start = ((), (), s32[]{:S(2)}) async-start(), calls=%async_computation.3 | async-start | bytes 1351680 | tf_op jit(solution)/shard_map/all_gather | solution.py:79
  12.8 57.8 %copy-start.2 = (bf16[2,32,576]{2,1,0:T(8,128)(2,1)S(1)}, bf16[2,32,576]{2,1,0:T(8,128)(2,1)}, u32[]{:S(2)}) copy-start(bf16[2,32,576]{2,1,0:T(8,128)(2,1)} %param.8) | copy-start | bytes 221188
  67.6 8.2 %copy-start.1 = (bf16[1024,576]{1,0:T(8,128)(2,1)S(1)}, bf16[1024,576]{1,0:T(8,128)(2,1)}, u32[]{:S(2)}) copy-start(bf16[1024,576]{1,0:T(8,128)(2,1)} %all-gather.2.cloned.1.call-done) | copy-start | bytes 3538948
  72.1 10.3 %all-to-all-start.1 = ((f32[1,2,32]{1,0,2:T(1,128)}), f32[1,2,32]{1,0,2:T(1,128)S(1)}, u32[]{:S(2)}, u32[]{:S(2)}) async-start(f32[1,2,32]{1,0,2:T(1,128)} %copy.21), calls=%async_computation.1 | async-start | bytes 32768 | tf_op jit(solution)/shard_map/all_to_all | solution.py:116
  82.4 12.6 %all-to-all-start.2 = ((f32[1,2,32]{1,0,2:T(1,128)}), f32[1,2,32]{1,0,2:T(1,128)S(1)}, u32[]{:S(2)}, u32[]{:S(2)}) async-start(f32[1,2,32]{1,0,2:T(1,128)} %copy.24), calls=%async_computation.2 | async-start | bytes 32768 | tf_op jit(solution)/shard_map/all_to_all | solution.py:117
  94.9 11.1 %all-to-all-start = ((f32[1,2,32,512]{3,1,0,2:T(2,128)}), f32[1,2,32,512]{3,1,0,2:T(2,128)S(1)}, u32[]{:S(2)}, u32[]{:S(2)}) async-start(f32[1,2,32,512]{3,1,0,2:T(2,128)} %copy.20), calls=%async_computation | async-start | bytes 262144 | tf_op jit(solution)/shard_map/all_to_all | solution.py:118
Sparse Core Ops, SparseCore 0:
  10.8 56.6 all-gather.1
where the time goes:
time: 114 us
  waiting for transfers between devices  67.7 us (59%)
  between operations  14.2 us (12%)
  starting transfers between devices  12.1 us (11%)
  matrix products  8.78 us (8%)
  local copies, waits for them, and re-layouts  6.53 us (6%)
  other arithmetic  4.37 us (4%)
    all_gather x1, waiting for transfers between devices, shards(): gathered = lax.all_gather(prefill_latent, 'ctx', axis=0, tiled=True)  54.8 us
    all_to_all x1, waiting for transfers between devices, shards(): lax.all_to_all(part_out[None], 'ctx', split_axis=2, concat_axis=0, tiled=...  7.87 us
    all_to_all x1, starting transfers between devices, shards(): lax.all_to_all(part_sum[None], 'ctx', split_axis=2, concat_axis=0, tiled=...  5.76 us
    all_to_all x1, waiting for transfers between devices, shards(): lax.all_to_all(part_sum[None], 'ctx', split_axis=2, concat_axis=0, tiled=...  4.27 us
    all_to_all x1, starting transfers between devices, shards(): lax.all_to_all(part_max[None], 'ctx', split_axis=2, concat_axis=0, tiled=...  3.51 us
    gather x1, local copies, waits for them, and re-layouts, pick_rows(): taken = jnp.take(shard_rows, jnp.clip(local_rows, 0, length - 1), axis=0)  2.89 us
    dot_general x2, matrix products, attend_block(): jnp.einsum('ihj,jv->ihv', weights.astype(jnp.bfloat16), shard_rows[:, :D_...  2.85 us
    all_to_all x1, starting transfers between devices, shards(): lax.all_to_all(part_out[None], 'ctx', split_axis=2, concat_axis=0, tiled=...  2.81 us
  transfers between devices with their start and end apart: 4, of which 4 were waited for; matrix products, arithmetic and copies ran while one was open for 13% of the time, Pallas kernels for 0%

commit v1 on v0

v1 whole, which is shorter than its diff:
```python
import functools

import jax
import jax.numpy as jnp
from jax import lax
from jax.experimental import pallas as pl
from jax.experimental.pallas import tpu as pltpu
from jax.sharding import PartitionSpec as P

D_LAT = 512
PAGE = 16
POOL = 16
REQ = 2

SCALE = 192.0 ** (-0.5)
NEG = -1e30
MSG = D_LAT + 128


def kernel(
    n,
    qt_hbm,
    lat_hbm,
    dq_ref,
    ct_hbm,
    len_ref,
    pt_ref,
    pout_ref,
    dout_ref,
    held,
    qt,
    q,
    ct,
    parts,
    moved,
    local_sem,
    z_sem,
    x_sem,
    y_sem,
    pair_sem,
    dx_sem,
    dy_sem,
    full_sem,
    half_sem,
    dsend_sem,
    drecv_sem,
):
    me = lax.axis_index("ctx")
    line = n // 8
    core = me % 2
    x = (me // 2) % 2
    y = (me // 4) % 2
    z = me // 8
    rows = lat_hbm.shape[0]
    heads = dq_ref.shape[1]
    span = qt.shape[1]
    cache_dev = ct.shape[2]

    def block(step, by, bx, bc):
        return ((((z + step) % line) * 2 + by) * 2 + bx) * 2 + bc

    def device(step, dy, dx, dc):
        return ((((z + line - step) % line) * 2 + dy) * 2 + dx) * 2 + dc

    x_peer = device(0, y, 1 - x, core)
    y_peer = device(0, 1 - y, x, core)
    pair = device(0, y, x, 1 - core)

    own_copy = pltpu.make_async_copy(lat_hbm, held.at[me], local_sem.at[0])
    own_copy.start()
    q_copy = pltpu.make_async_copy(qt_hbm, qt, local_sem.at[1])
    q_copy.start()
    c_copy = pltpu.make_async_copy(ct_hbm, ct, local_sem.at[2])
    c_copy.start()

    barrier = pltpu.get_barrier_semaphore()

    def greet(step, carry):
        pl.semaphore_signal(barrier, inc=1, device_id={"ctx": (me + step) % n})
        return carry

    lax.fori_loop(1, n, greet, 0)

    split = rows // 2 if rows % 32 == 0 else rows

    def move(index, send, recv, target, part=None):
        ref = held.at[index]
        if part == 0:
            ref = held.at[index, pl.ds(0, split)]
        if part == 1:
            ref = held.at[index, pl.ds(split, rows - split)]
        return pltpu.make_async_remote_copy(
            src_ref=ref, dst_ref=ref, send_sem=send, recv_sem=recv, device_id={"ctx": target}
        )

    sends = []

    def go(copy):
        copy.start()
        sends.append(copy)

    def to_pair(step, by, bx):
        index = block(step, by, bx, core)
        spot = (step * 2 + (0 if by is y else 1)) * 2 + (0 if bx is x else 1)
        go(move(index, pair_sem.at[spot], full_sem.at[index], pair))

    def full_wait(index):
        move(index, z_sem.at[0], full_sem.at[index], pair).wait_recv()

    def half_wait(index):
        move(index, z_sem.at[0], half_sem.at[index, 0], pair, 0).wait_recv()
        if split < rows:
            move(index, z_sem.at[0], half_sem.at[index, 1], pair, 1).wait_recv()

    far_x, far_y = 1 - x, 1 - y

    def spread_column(step):
        index = block(step, y, x, core)
        go(move(index, x_sem.at[step], full_sem.at[index], x_peer))
        go(move(index, y_sem.at[step], full_sem.at[index], y_peer))
        to_pair(step, y, x)

    def spread_plane(step):
        index = block(step, y, far_x, core)
        full_wait(index)
        if split < rows:
            go(move(index, dy_sem.at[step], half_sem.at[index, 1], y_peer, 1))
        to_pair(step, y, far_x)
        index = block(step, far_y, x, core)
        full_wait(index)
        go(move(index, dx_sem.at[step], half_sem.at[index, 0], x_peer, 0))
        to_pair(step, far_y, x)

    own_copy.wait()
    pl.semaphore_wait(barrier, n - 1)

    for step in range(line - 1, 0, -1):
        go(move(me, z_sem.at[step], full_sem.at[me], device(step, y, x, core)))
    spread_column(0)

    c_copy.wait()
    latent = held[me]
    row_page = (me * rows + lax.broadcasted_iota(jnp.int32, (1, rows), 1)) // PAGE
    first_page = me * rows // PAGE
    request_of = jnp.zeros((1, rows), jnp.int32)
    for p in range(max(1, rows // PAGE)):
        page = first_page + p
        request = (pt_ref[0, page] * POOL + pt_ref[1, page]) % REQ
        request_of = jnp.where(row_page == page, request, request_of)
    positions = me * cache_dev + lax.broadcasted_iota(jnp.int32, (1, cache_dev), 1)
    nt = (((1,), (1,)), ((), ()))
    for r in range(REQ):
        queries = dq_ref[r]
        keys = ct[r]
        scores = jnp.dot(queries, keys, preferred_element_type=jnp.float32) * SCALE
        page_scores = (
            lax.dot_general(queries, latent, nt, preferred_element_type=jnp.float32) * SCALE
        )
        ok = positions < len_ref[r]
        page_ok = request_of == r
        scores = jnp.where(ok, scores, NEG)
        page_scores = jnp.where(page_ok, page_scores, NEG)
        top = jnp.maximum(
            jnp.max(scores, axis=1, keepdims=True), jnp.max(page_scores, axis=1, keepdims=True)
        )
        weights = jnp.where(ok, jnp.exp(scores - top), 0.0)
        page_weights = jnp.where(page_ok, jnp.exp(page_scores - top), 0.0)
        total = jnp.sum(weights, axis=1, keepdims=True) + jnp.sum(
            page_weights, axis=1, keepdims=True
        )
        mixed = lax.dot_general(
            weights.astype(jnp.bfloat16), keys[:D_LAT], nt, preferred_element_type=jnp.float32
        ) + jnp.dot(
            page_weights.astype(jnp.bfloat16),
            latent[:, :D_LAT],
            preferred_element_type=jnp.float32,
        )
        lane = lax.broadcasted_iota(jnp.int32, (heads, 128), 1)
        tail = jnp.where(lane < 64, top, total)
        parts[:, :, r * MSG : r * MSG + D_LAT] = mixed.reshape(heads, 1, D_LAT)
        parts[:, :, r * MSG + D_LAT : (r + 1) * MSG] = tail.reshape(heads, 1, 128)

    def part_copy(target, source, step):
        return pltpu.make_async_remote_copy(
            src_ref=parts.at[target],
            dst_ref=moved.at[source],
            send_sem=dsend_sem.at[step],
            recv_sem=drecv_sem.at[source],
            device_id={"ctx": target},
        )

    moved[me] = parts[me]

    def send_part(step, carry):
        part_copy((me + step) % n, me, step).start()
        return carry

    lax.fori_loop(1, n, send_part, 0)

    spread_plane(0)
    q_copy.wait()
    for start in range(0, span, 128):
        q[start : start + 128, :] = qt[:, start : start + 128].T
    for step in range(1, line):
        full_wait(block(step, y, x, core))
        spread_column(step)
    for step in range(1, line):
        spread_plane(step)
    for step in range(line):
        half_wait(block(step, far_y, far_x, core))
        to_pair(step, far_y, far_x)
    for step in range(line):
        for by in (y, far_y):
            for bx in (x, far_x):
                full_wait(block(step, by, bx, 1 - core))

    chunk = min(256, span)
    for start in range(0, span, chunk):
        stop = start + chunk
        keys = held[: stop // rows].reshape(stop, held.shape[2])
        scores = lax.dot_general(
            q[start:stop], keys, nt, preferred_element_type=jnp.float32
        )
        row = start + lax.broadcasted_iota(jnp.int32, (chunk, stop), 0)
        col = lax.broadcasted_iota(jnp.int32, (chunk, stop), 1)
        scores = jnp.where(col <= row, scores, NEG)
        top = jnp.max(scores, axis=1, keepdims=True)
        weights = jnp.exp((scores - top) * SCALE)
        total = jnp.sum(weights, axis=1, keepdims=True)
        mixed = jnp.dot(
            weights.astype(jnp.bfloat16), keys[:, :D_LAT], preferred_element_type=jnp.float32
        )
        pout_ref[start:stop, :] = (mixed / total).astype(jnp.bfloat16)

    def await_part(step, carry):
        part_copy((me + step) % n, (me + step) % n, step).wait_recv()
        return carry

    lax.fori_loop(1, n, await_part, 0)
    for r in range(REQ):
        piece = moved[:, :, r * MSG : (r + 1) * MSG].reshape(n, MSG)
        tops = piece[:, D_LAT : D_LAT + 1]
        sums = piece[:, D_LAT + 64 : D_LAT + 65]
        factor = jnp.exp(tops - jnp.max(tops, axis=0, keepdims=True))
        own_sum = jnp.sum(sums * factor, axis=0, keepdims=True)
        own_out = jnp.sum(piece[:, :D_LAT] * factor, axis=0, keepdims=True)
        dout_ref[r : r + 1, :] = (own_out / own_sum).astype(jnp.bfloat16)

    for copy in sends:
        copy.wait_send()

    def drain(step, carry):
        part_copy((me + step) % n, me, step).wait_send()
        return carry

    lax.fori_loop(1, n, drain, 0)


def shards(n, prefill_query, prefill_latent, decode_query, cache, lengths, page_table):
    span, head_here, width = prefill_query.shape
    rows = prefill_latent.shape[0]
    heads = decode_query.shape[1]
    cache_dev = cache.shape[1]
    if head_here != 1 or n % 8 or rows * n != span:
        raise ValueError("unexpected sizes")
    line = n // 8
    vmem = pl.BlockSpec(memory_space=pltpu.VMEM)
    smem = pl.BlockSpec(memory_space=pltpu.SMEM)
    anywhere = pl.BlockSpec(memory_space=pl.ANY)
    dma = pltpu.SemaphoreType.DMA
    prefill_out, decode_out = pl.pallas_call(
        functools.partial(kernel, n),
        out_shape=(
            jax.ShapeDtypeStruct((span, D_LAT), jnp.bfloat16),
            jax.ShapeDtypeStruct((REQ, D_LAT), jnp.bfloat16),
        ),
        in_specs=[anywhere, anywhere, vmem, anywhere, smem, smem],
        out_specs=(vmem, vmem),
        scratch_shapes=[
            pltpu.VMEM((n, rows, width), jnp.bfloat16),
            pltpu.VMEM((width, span), jnp.bfloat16),
            pltpu.VMEM((span, width), jnp.bfloat16),
            pltpu.VMEM((REQ, width, cache_dev), jnp.bfloat16),
            pltpu.VMEM((heads, 1, REQ * MSG), jnp.float32),
            pltpu.VMEM((n, 1, REQ * MSG), jnp.float32),
            dma((3,)),
            dma((line,)),
            dma((line,)),
            dma((line,)),
            dma((line * 4,)),
            dma((line,)),
            dma((line,)),
            dma((n,)),
            dma((n, 2)),
            dma((n,)),
            dma((n,)),
        ],
        compiler_params=pltpu.CompilerParams(collective_id=0, has_side_effects=True),
    )(
        prefill_query[:, 0, :].T,
        prefill_latent,
        decode_query,
        jnp.swapaxes(cache, 1, 2),
        lengths,
        page_table.T,
    )
    return prefill_out[:, None, :], decode_out[:, None, :]


def solution(mesh):
    in_specs = (
        P("groups", "ctx", None),
        P(("groups", "ctx"), None),
        P("groups", None, None),
        P("groups", "ctx", None),
        P("groups"),
        P("groups", None),
    )
    out_specs = (P("groups", "ctx", None), P("groups", "ctx", None))
    return jax.shard_map(
        functools.partial(shards, mesh.shape["ctx"]),
        mesh=mesh,
        in_specs=in_specs,
        out_specs=out_specs,
        check_vma=False,
    )
```

time: 114 us -> 32 us (0.28)
  the two profiles are of different devices: /device:TPU:1 before, /device:TPU:9 now
where the time goes in v1:
time: 32 us; the launch traced here: 31.8 us
  Pallas kernels  28.4 us (89%)
  local copies, waits for them, and re-layouts  2.84 us (9%)
  between operations  0.65 us (2%)
    pallas_call x1, Pallas kernels, shards(): pl.pallas_call(functools.partial(kernel, n), out_shape=(jax.ShapeDtypeStr...  28.4 us
    unnamed x4, local copies, waits for them, and re-layouts  2.84 us

profile of v1, /device:TPU:9, one launch (start us, length us, event | category | flops | bytes accessed | tf_op | source)
XLA Modules:
  0.0 31.8 jit_solution(1739083343625715405)
XLA Ops:
  0.6 28.4 %shard_map.77 = (bf16[1024,512]{1,0:T(8,128)(2,1)}, bf16[2,512]{1,0:T(2,128)(2,1)}) custom-call(bf16[576,1024]{1,0:T(8,128)(2,1)} %bitcast.7, bf16[32,576]{1,0:T(8,128)(2,1)} %lat_hbm.1, bf16[2,32,576]{2,1,0:T(8,128)(2,1)} %dq_ref.1, bf16[2,576,512]{2,1,0:T(8,128)(2,1)} %bitcast.8, s32[2]{0:T(128)} %len_ref.1, s32[2,64]{1,0:T(2,128)} %bitcast.11), custom_call_target="tpu_custom_call" | custom-call | tf_op jit(solution)/shard_map/pallas_call | solution.py:271
  29.0 0.0 copy-start
  29.0 2.3 %copy.10 = bf16[1024,1,512]{2,0,1:T(8,128)(2,1)} copy(bf16[1024,1,512]{2,0,1:T(8,128)(2,1)} %bitcast.9) | data formatting | bytes 2097152
  31.3 0.0 copy-done
  31.3 0.6 %copy.11 = bf16[2,1,512]{2,0,1:T(2,128)(2,1)} copy(bf16[2,1,512]{2,0,1:T(2,128)(2,1)S(1)} %bitcast.10) | data formatting | bytes 4096
Async XLA Ops:
  29.0 2.3 %copy-start = (bf16[2,512]{1,0:T(2,128)(2,1)S(1)}, bf16[2,512]{1,0:T(2,128)(2,1)}, u32[]{:S(2)}) copy-start(bf16[2,512]{1,0:T(2,128)(2,1)} %get-tuple-element.5) | copy-start | bytes 6148

commit v2 on v1

--- a/solution.py
+++ b/solution.py
@@ -21,17 +21,20 @@
     n,
     qt_hbm,
     lat_hbm,
-    dq_ref,
+    dq_hbm,
     ct_hbm,
     len_ref,
     pt_ref,
     pout_ref,
     dout_ref,
     held,
+    dq_ref,
     qt,
     q,
     ct,
     parts,
+    mate,
+    joined,
     moved,
     local_sem,
     z_sem,
@@ -44,6 +47,8 @@
     half_sem,
     dsend_sem,
     drecv_sem,
+    ready_sem,
+    mate_sem,
 ):
     me = lax.axis_index("ctx")
     line = n // 8
@@ -53,18 +58,26 @@
     z = me // 8
     rows = lat_hbm.shape[0]
     heads = dq_ref.shape[1]
+    chips = n // 2
     span = qt.shape[1]
     cache_dev = ct.shape[2]
 
+    def opposite(step):
+        result, bit = z, 1
+        while bit <= step:
+            if step // bit % 2:
+                result = result + bit * (1 - 2 * (z // bit % 2))
+            bit *= 2
+        return result
+
+    lines = [opposite(step) for step in range(line)]
+
     def block(step, by, bx, bc):
-        return ((((z + step) % line) * 2 + by) * 2 + bx) * 2 + bc
-
-    def device(step, dy, dx, dc):
-        return ((((z + line - step) % line) * 2 + dy) * 2 + dx) * 2 + dc
-
-    x_peer = device(0, y, 1 - x, core)
-    y_peer = device(0, 1 - y, x, core)
-    pair = device(0, y, x, 1 - core)
+        return ((lines[step] * 2 + by) * 2 + bx) * 2 + bc
+
+    x_peer = block(0, y, 1 - x, core)
+    y_peer = block(0, 1 - y, x, core)
+    pair = block(0, y, x, 1 - core)
 
     own_copy = pltpu.make_async_copy(lat_hbm, held.at[me], local_sem.at[0])
     own_copy.start()
@@ -72,14 +85,14 @@
     q_copy.start()
     c_copy = pltpu.make_async_copy(ct_hbm, ct, local_sem.at[2])
     c_copy.start()
+    d_copy = pltpu.make_async_copy(dq_hbm, dq_ref, local_sem.at[3])
+    d_copy.start()
 
     barrier = pltpu.get_barrier_semaphore()
 
-    def greet(step, carry):
-        pl.semaphore_signal(barrier, inc=1, device_id={"ctx": (me + step) % n})
-        return carry
-
-    lax.fori_loop(1, n, greet, 0)
+    near = [x_peer, y_peer, pair] + [block(step, y, x, core) for step in range(1, line)]
+    for target in near:
+        pl.semaphore_signal(barrier, inc=1, device_id={"ctx": target})
 
     split = rows // 2 if rows % 32 == 0 else rows
 
@@ -131,14 +144,18 @@
         go(move(index, dx_sem.at[step], half_sem.at[index, 0], x_peer, 0))
         to_pair(step, far_y, x)
 
+    q_copy.wait()
+    for start in range(0, span, 128):
+        q[start : start + 128, :] = qt[:, start : start + 128].T
     own_copy.wait()
-    pl.semaphore_wait(barrier, n - 1)
-
-    for step in range(line - 1, 0, -1):
-        go(move(me, z_sem.at[step], full_sem.at[me], device(step, y, x, core)))
+    pl.semaphore_wait(barrier, len(near))
+
+    pl.semaphore_signal(ready_sem.at[0], inc=1, device_id={"ctx": x_peer})
     spread_column(0)
-
+    for step in range(1, line):
+        go(move(me, z_sem.at[step], full_sem.at[me], block(step, y, x, core)))
     c_copy.wait()
+    d_copy.wait()
     latent = held[me]
     row_page = (me * rows + lax.broadcasted_iota(jnp.int32, (1, rows), 1)) // PAGE
     first_page = me * rows // PAGE
@@ -177,42 +194,71 @@
         )
         lane = lax.broadcasted_iota(jnp.int32, (heads, 128), 1)
         tail = jnp.where(lane < 64, top, total)
-        parts[:, :, r * MSG : r * MSG + D_LAT] = mixed.reshape(heads, 1, D_LAT)
-        parts[:, :, r * MSG + D_LAT : (r + 1) * MSG] = tail.reshape(heads, 1, 128)
-
-    def part_copy(target, source, step):
+        parts[:, :, :, r * MSG : r * MSG + D_LAT] = mixed.reshape(chips, 2, 1, D_LAT)
+        parts[:, :, :, r * MSG + D_LAT : (r + 1) * MSG] = tail.reshape(chips, 2, 1, 128)
+
+    mate_copy = pltpu.make_async_remote_copy(
+        src_ref=parts.at[:, 1 - core],
+        dst_ref=mate,
+        send_sem=mate_sem.at[0],
+        recv_sem=mate_sem.at[1],
+        device_id={"ctx": pair},
+    )
+    mate_copy.start()
+
+    def part_copy(target, source):
         return pltpu.make_async_remote_copy(
-            src_ref=parts.at[target],
+            src_ref=joined.at[target],
             dst_ref=moved.at[source],
-            send_sem=dsend_sem.at[step],
+            send_sem=dsend_sem.at[target],
             recv_sem=drecv_sem.at[source],
-            device_id={"ctx": target},
-        )
-
-    moved[me] = parts[me]
+            device_id={"ctx": target * 2 + core},
+        )
+
+    chip = me // 2
+
+    def ready(stage, target):
+        pl.semaphore_signal(ready_sem.at[stage], inc=1, device_id={"ctx": target})
 
     def send_part(step, carry):
-        part_copy((me + step) % n, me, step).start()
+        part_copy((chip + step) % chips, chip).start()
         return carry
 
-    lax.fori_loop(1, n, send_part, 0)
-
+    def join():
+        mate_copy.wait_recv()
+        for r in range(REQ):
+            mine = parts[:, core, :, r * MSG : (r + 1) * MSG].reshape(chips, MSG)
+            other = mate[:, :, r * MSG : (r + 1) * MSG].reshape(chips, MSG)
+            top_mine = mine[:, D_LAT : D_LAT + 1]
+            top_other = other[:, D_LAT : D_LAT + 1]
+            top = jnp.maximum(top_mine, top_other)
+            both = mine * jnp.exp(top_mine - top) + other * jnp.exp(top_other - top)
+            lane = lax.broadcasted_iota(jnp.int32, (chips, 128), 1)
+            tail = jnp.where(lane < 64, top, both[:, D_LAT:])
+            joined[:, :, r * MSG : r * MSG + D_LAT] = both[:, :D_LAT].reshape(chips, 1, D_LAT)
+            joined[:, :, r * MSG + D_LAT : (r + 1) * MSG] = tail.reshape(chips, 1, 128)
+        moved[chip] = joined[chip]
+
+    pl.semaphore_wait(ready_sem.at[0], 1)
+    ready(1, y_peer)
     spread_plane(0)
-    q_copy.wait()
-    for start in range(0, span, 128):
-        q[start : start + 128, :] = qt[:, start : start + 128].T
+    join()
+    pl.semaphore_wait(ready_sem.at[1], 1)
+    lax.fori_loop(1, chips, send_part, 0)
     for step in range(1, line):
         full_wait(block(step, y, x, core))
         spread_column(step)
     for step in range(1, line):
         spread_plane(step)
     for step in range(line):
-        half_wait(block(step, far_y, far_x, core))
+        index = block(step, far_y, far_x, core)
+        half_wait(index)
         to_pair(step, far_y, far_x)
     for step in range(line):
         for by in (y, far_y):
             for bx in (x, far_x):
-                full_wait(block(step, by, bx, 1 - core))
+                index = block(step, by, bx, 1 - core)
+                full_wait(index)
 
     chunk = min(256, span)
     for start in range(0, span, chunk):
@@ -233,12 +279,13 @@
         pout_ref[start:stop, :] = (mixed / total).astype(jnp.bfloat16)
 
     def await_part(step, carry):
-        part_copy((me + step) % n, (me + step) % n, step).wait_recv()
+        source = (chip + step) % chips
+        part_copy(source, source).wait_recv()
         return carry
 
-    lax.fori_loop(1, n, await_part, 0)
+    lax.fori_loop(1, chips, await_part, 0)
     for r in range(REQ):
-        piece = moved[:, :, r * MSG : (r + 1) * MSG].reshape(n, MSG)
+        piece = moved[:, :, r * MSG : (r + 1) * MSG].reshape(chips, MSG)
         tops = piece[:, D_LAT : D_LAT + 1]
         sums = piece[:, D_LAT + 64 : D_LAT + 65]
         factor = jnp.exp(tops - jnp.max(tops, axis=0, keepdims=True))
@@ -250,10 +297,11 @@
         copy.wait_send()
 
     def drain(step, carry):
-        part_copy((me + step) % n, me, step).wait_send()
+        part_copy((chip + step) % chips, chip).wait_send()
         return carry
 
-    lax.fori_loop(1, n, drain, 0)
+    mate_copy.wait_send()
+    lax.fori_loop(1, chips, drain, 0)
 
 
 def shards(n, prefill_query, prefill_latent, decode_query, cache, lengths, page_table):
@@ -271,19 +319,23 @@
     prefill_out, decode_out = pl.pallas_call(
         functools.partial(kernel, n),
         out_shape=(
-            jax.ShapeDtypeStruct((span, D_LAT), jnp.bfloat16),
-            jax.ShapeDtypeStruct((REQ, D_LAT), jnp.bfloat16),
+            pltpu.VMEM((span, D_LAT), jnp.bfloat16),
+            pltpu.VMEM((REQ, D_LAT), jnp.bfloat16),
         ),
-        in_specs=[anywhere, anywhere, vmem, anywhere, smem, smem],
+        in_specs=[anywhere, anywhere, anywhere, anywhere, smem, smem],
         out_specs=(vmem, vmem),
         scratch_shapes=[
             pltpu.VMEM((n, rows, width), jnp.bfloat16),
+            pltpu.VMEM((REQ, heads, width), jnp.bfloat16),
             pltpu.VMEM((width, span), jnp.bfloat16),
             pltpu.VMEM((span, width), jnp.bfloat16),
             pltpu.VMEM((REQ, width, cache_dev), jnp.bfloat16),
-            pltpu.VMEM((heads, 1, REQ * MSG), jnp.float32),
-            pltpu.VMEM((n, 1, REQ * MSG), jnp.float32),
-            dma((3,)),
+            pltpu.VMEM((n // 2, 2, 1, REQ * MSG), jnp.float32),
+            pltpu.VMEM((n // 2, 1, REQ * MSG), jnp.float32),
+            pltpu.VMEM((n // 2, 1, REQ * MSG), jnp.float32),
+            pltpu.VMEM((n // 2, 1, REQ * MSG), jnp.float32),
+
+            dma((4,)),
             dma((line,)),
             dma((line,)),
             dma((line,)),
@@ -292,8 +344,10 @@
             dma((line,)),
             dma((n,)),
             dma((n, 2)),
-            dma((n,)),
-            dma((n,)),
+            dma((n // 2,)),
+            dma((n // 2,)),
+            pltpu.SemaphoreType.REGULAR((2,)),
+            dma((2,)),
         ],
         compiler_params=pltpu.CompilerParams(collective_id=0, has_side_effects=True),
     )(

time: 32 us -> 26.4 us (0.82)
  the two profiles are of different devices: /device:TPU:9 before, /device:TPU:1 now
where the time goes in v2:
time: 26.4 us; the launch traced here: 26.3 us
  Pallas kernels  24.1 us (91%)
  local copies, waits for them, and re-layouts  1.55 us (6%)
  between operations  0.64 us (2%)
    pallas_call x1, Pallas kernels, shards(): pl.pallas_call(functools.partial(kernel, n), out_shape=(pltpu.VMEM((span,...  24.1 us
    unnamed x2, local copies, waits for them, and re-layouts  1.55 us

profile of v2, /device:TPU:1, one launch (start us, length us, event | category | flops | bytes accessed | tf_op | source)
XLA Modules:
  0.0 26.3 jit_solution(13020431505055458695)
XLA Ops:
  0.6 24.1 %shard_map.77 = (bf16[1024,512]{1,0:T(8,128)(2,1)S(1)}, bf16[2,512]{1,0:T(2,128)(2,1)S(1)}) custom-call(bf16[576,1024]{1,0:T(8,128)(2,1)} %bitcast.9, bf16[32,576]{1,0:T(8,128)(2,1)} %lat_hbm.1, bf16[2,32,576]{2,1,0:T(8,128)(2,1)} %dq_hbm.1, bf16[2,576,512]{2,1,0:T(8,128)(2,1)} %bitcast.10, s32[2]{0:T(128)} %len_ref.1, s32[2,64]{1,0:T(2,128)} %bitcast.11), custom_call_target="tpu_custom_call" | custom-call | tf_op jit(solution)/shard_map/pallas_call | solution.py:319
  24.7 1.0 %copy.10 = bf16[1024,1,512]{2,0,1:T(8,128)(2,1)} copy(bf16[1024,1,512]{2,0,1:T(8,128)(2,1)S(1)} %bitcast.7) | data formatting | bytes 2097152
  25.7 0.6 %copy.11 = bf16[2,1,512]{2,0,1:T(2,128)(2,1)} copy(bf16[2,1,512]{2,0,1:T(2,128)(2,1)S(1)} %bitcast.8) | data formatting | bytes 4096
